TPU v7x, 256 devices: a whole 4x4x8 slice. The times are simulated.
256 devices in a mesh: ctx: 32 (over y_hi, z, core), tp: 8 (over y_lo, x).
Axes of the slice: x: 4, y: 4 (y_hi: 2, y_lo: 2; y = y_hi * 2 + y_lo), z: 8, core: 2. Of those that a mesh axis runs over, the one named last changes fastest.
Arguments:
- tokens: bfloat16 [8192, 8192], P(('ctx', 'tp')), may hold values from -64 to 64
- query_weight: bfloat16 [8192, 4096], P(None, 'tp'), may hold values from -0.0625 to 0.0625
- keyval_weight: bfloat16 [8192, 2048], P(None, 'tp'), may hold values from -0.0625 to 0.0625
- doc_lengths: int32 [64], replicated, may hold values from 1 to 2048, 8192 in all
- owners: int32 [512], replicated, may hold values from 0 to 31, as said below
Outputs:
- attended: bfloat16 [8192, 4096], P('ctx', 'tp')
Inputs may be any that keep to these rules, and one draw needn't show every extreme that they name: The 16 blocks of one index of ctx (blocks i * 16 to (i + 1) * 16 - 1) go to 16 different owners; for each position j < 16, the blocks i * 16 + j of all indices i go to all different owners, so every owner receives exactly one block of each position.
All inputs are finite; a program needn't handle non-finite values.
Results may differ from a plain program's by a relative error of at most 0.0055.
The roundings to bfloat16 on the way count: a program that leaves them out, or rounds other values in their place, can miss the bound.
Values may be sent and summed in bfloat16 or wider, within the bound.
A program may use at most 128 MiB of HBM per device.

v0:
```python
import math
import jax
import jax.numpy as jnp
from jax import lax
from jax.sharding import PartitionSpec as P

NEG_FILL = -1e30


def token_places(block_order, first_row, row_count, block_len):
    row_index = first_row + jnp.arange(row_count, dtype=jnp.int32)
    return block_order[row_index // block_len] * block_len + row_index % block_len


def documents(token_place, doc_ends):
    return jnp.sum((doc_ends[None, :] <= token_place[:, None]).astype(jnp.int32), axis=1)


def body(tokens, query_weight, keyval_weight, doc_lengths, owners):
    cycle_count = lax.axis_size("ctx")
    device = lax.axis_index("ctx")
    group_count = lax.axis_size("tp")
    share_rows = tokens.shape[0]
    tok_rows = share_rows * group_count
    per_device = owners.shape[0] // cycle_count
    block_len = tok_rows // per_device
    head_dim = keyval_weight.shape[1] // 2
    query_cols = query_weight.shape[1]
    block_order = jnp.argsort(owners, stable=True)
    doc_ends = jnp.cumsum(doc_lengths)
    owner_grid = owners.reshape(cycle_count, per_device)
    own_targets = lax.dynamic_index_in_dim(owner_grid, device, 0, keepdims=False)
    piece = lax.all_gather(tokens, "tp", axis=0, tiled=True)
    query_part = jnp.dot(piece, query_weight, preferred_element_type=jnp.float32).astype(
        jnp.bfloat16
    )
    keyval_part = jnp.dot(piece, keyval_weight, preferred_element_type=jnp.float32).astype(
        jnp.bfloat16
    )
    projected = jnp.concatenate([query_part, keyval_part], axis=1)
    columns = projected.shape[1]
    blocks = projected.reshape(own_targets.shape[0], block_len, columns)
    arrived = lax.all_to_all(
        jnp.zeros((cycle_count, block_len, columns), projected.dtype).at[own_targets].set(blocks),
        "ctx",
        split_axis=0,
        concat_axis=0,
        tiled=True,
    )
    sources = jnp.nonzero(owners == device, size=per_device)[0] // per_device
    projected = arrived[sources].reshape(tok_rows, arrived.shape[2])
    queries = projected[:, :query_cols]
    keyvals = projected[:, query_cols:]
    heads_here = query_cols // head_dim
    score_scale = 1.0 / math.sqrt(head_dim)
    query_heads = queries.reshape(tok_rows, heads_here, head_dim).transpose(1, 0, 2)
    query_place = token_places(block_order, device * tok_rows, tok_rows, block_len)
    query_docs = documents(query_place, doc_ends)
    initial = (
        jnp.full((heads_here, tok_rows), NEG_FILL, jnp.float32),
        jnp.zeros((heads_here, tok_rows), jnp.float32),
        jnp.zeros((heads_here, tok_rows, head_dim), jnp.float32),
    )
    key_piece = lax.all_gather(keyvals, "ctx", axis=0, tiled=True)
    count_rows = key_piece.shape[0]
    sub_rows = math.gcd(count_rows, 512)
    key_place = token_places(block_order, jnp.int32(0), count_rows, block_len)
    key_docs = documents(key_place, doc_ends)
    stacked = (
        key_piece.reshape(count_rows // sub_rows, sub_rows, key_piece.shape[1]),
        key_place.reshape(count_rows // sub_rows, sub_rows),
        key_docs.reshape(count_rows // sub_rows, sub_rows),
    )

    def advance(partial_value, member):
        keyval, member_place, member_docs = member
        allowed = (member_docs[None, :] == query_docs[:, None]) & (
            member_place[None, :] <= query_place[:, None]
        )

        def update(current):
            run_max, run_sum, run_acc = current
            scores = (
                jnp.einsum(
                    "hqd,kd->hqk",
                    query_heads,
                    keyval[:, :head_dim],
                    preferred_element_type=jnp.float32,
                )
                * score_scale
            )
            scores = jnp.where(allowed[None], scores, NEG_FILL)
            new_max = jnp.maximum(run_max, jnp.max(scores, axis=2))
            weights = jnp.where(allowed[None], jnp.exp(scores - new_max[:, :, None]), 0.0)
            factor = jnp.exp(run_max - new_max)
            new_sum = run_sum * factor + jnp.sum(weights, axis=2)
            new_acc = run_acc * factor[:, :, None] + jnp.einsum(
                "hqk,kd->hqd",
                weights.astype(jnp.bfloat16),
                keyval[:, head_dim:],
                preferred_element_type=jnp.float32,
            )
            return (new_max, new_sum, new_acc)

        def unchanged(current):
            return current

        return (lax.cond(jnp.any(allowed), update, unchanged, partial_value), None)

    finished, unused = lax.scan(advance, initial, stacked)
    attended = finished[2] / finished[1][:, :, None]
    return attended.transpose(1, 0, 2).reshape(tok_rows, heads_here * head_dim).astype(jnp.bfloat16)


def solution(mesh):
    return jax.shard_map(
        body,
        mesh=mesh,
        in_specs=(P(("ctx", "tp"), None), P(None, "tp"), P(None, "tp"), P(), P()),
        out_specs=P("ctx", "tp"),
        check_vma=False,
    )
```

profile of v0, /device:TPU:1, one launch (start us, length us, event | category | flops | bytes accessed | tf_op | source)
XLA Modules:
  0.0 275.2 jit_solution(502739521675465678)
XLA Ops:
  8.2 59.6 %all-gather.3.cloned.1.call-done = bf16[256,8192]{1,0:T(8,128)(2,1)} async-done(((bf16[32,8192]{1,0:T(8,128)(2,1)}), bf16[256,8192]{1,0:T(8,128)(2,1)}) %all-gather.3.cloned.1.call-update) | async-done | bytes 4194320 | tf_op jit(solution)/shard_map/all_gather | solution.py:33
  67.8 7.1 %convolution_convert_fusion = bf16[256,512]{1,0:T(8,128)(2,1)S(1)} fusion(bf16[256,8192]{1,0:T(8,128)(2,1)} %all-gather.3.cloned.1.call-done, bf16[8192,512]{1,0:T(8,128)(2,1)} %param.10), kind=kOutput, calls=%fused_computation.28 | convolution fusion | flops 2147614720 | bytes 12845056 | tf_op jit(solution)/shard_map/dot_general | solution.py:34
  75.0 1.2 convolution_convert_fusion.1
  76.3 0.9 broadcast_in_dim.60
  77.2 2.5 scatter_fusion
  79.7 10.1 %all-to-all-start = ((bf16[32,16,768]{2,1,0:T(8,128)(2,1)}), bf16[32,16,768]{2,1,0:T(8,128)(2,1)S(1)}, u32[]{:S(2)}, u32[]{:S(2)}) async-start(bf16[32,16,768]{2,1,0:T(8,128)(2,1)} %scatter_fusion), calls=%async_computation | async-start | bytes 1572864 | tf_op jit(solution)/shard_map/all_to_all | solution.py:43
  91.2 4.1 %scatter_custom_fusion.1 = s32[16]{0:T(128)S(1)} fusion(s32[512]{0:T(512)S(1)} %bitcast.63, s32[512]{0:T(512)S(1)} %broadcast.398, s32[]{:T(128)} %copy.68), kind=kCustom, calls=%fused_computation.89 | custom fusion | flops 512 | bytes 68 | tf_op jit(solution)/shard_map/scatter-add | solution.py:50
  96.2 16.5 %all-to-all-done = bf16[32,16,768]{2,1,0:T(8,128)(2,1)S(1)} async-done(((bf16[32,16,768]{2,1,0:T(8,128)(2,1)}), bf16[32,16,768]{2,1,0:T(8,128)(2,1)S(1)}, u32[]{:S(2)}, u32[]{:S(2)}) %all-to-all-start) | async-done | bytes 786464 | tf_op jit(solution)/shard_map/all_to_all | solution.py:43
  114.3 3.8 %sort.17 = (s32[512]{0:T(512)}, s32[512]{0:T(512)S(1)}) sort(s32[512]{0:T(512)S(1)} %copy-done, s32[512]{0:T(512)S(1)} %iota.37), dimensions={0}, to_apply=%region_6.7 | sort | flops 4608 | bytes 8192 | tf_op jit(solution)/shard_map/jit(argsort)/sort | solution.py:29
  118.1 1.9 gather_fusion.1
  120.1 51.2 %gather_fusion = s32[8192]{0:T(1024)S(1)} fusion(s32[512]{0:T(512)S(1)} %get-tuple-element.106, s32[8192]{0:T(1024)S(1)} %broadcast_clamp_fusion), kind=kCustom, calls=%fused_computation | custom fusion | bytes 98304 | tf_op jit(solution)/shard_map/gather | solution.py:12
  172.2 23.5 %all-gather.5.cloned.1.call-done = bf16[8192,256]{1,0:T(8,128)(2,1)} async-done(((bf16[256,256]{1,0:T(8,128)(2,1)}), bf16[8192,256]{1,0:T(8,128)(2,1)}) %all-gather.5.cloned.1.call-update) | async-done | bytes 4194320 | tf_op jit(solution)/shard_map/all_gather | solution.py:64
  195.7 71.7 %while.14 = (s32[]{:T(128)}, f32[4,256]{1,0:T(4,128)S(1)}, f32[4,256]{1,0:T(4,128)S(1)}, f32[4,256,128]{2,1,0:T(8,128)S(1)}, s32[16,512]{1,0:T(8,128)S(1)}, /*in...) while((s32[]{:T(128)}, f32[4,256]{1,0:T(4,128)S(1)}, ...), condition=%wide.region_16.17_spmd, body=%wide.region_10.16_spmd.sunk | while | flops 276039680 | bytes 8993003 | solution.py:110
  197.2 2.9 %conditional.2 = ((f32[4,256]{1,0:T(4,128)S(1)}, f32[4,256]{1,0:T(4,128)S(1)}, f32[4,256,128]{2,1,0:T(8,128)S(1)})) conditional(s32[]{:T(128)} %convert_element_type.54, (f32[4,256]{1,0:T(4,128)S(1)}, f32[4,256]{1,0:T(4,128)S(1)}, f32[4,256,128]{2,1,0:T(8,128)S(1)}) %tuple.42, (pred[256,512]{0,1:T(8,128)(4,1)S(1)}, ...), branch_computations={%region_12.12_spmd, %region_13.15_spmd} | conditional | flops 275515392 | bytes 8847396 | solution.py:108
  197.3 1.0 dynamic-slice_bitcast_fusion
  199.3 0.9 convolution_add_fusion
  201.7 2.9 %conditional.2 = ((f32[4,256]{1,0:T(4,128)S(1)}, f32[4,256]{1,0:T(4,128)S(1)}, f32[4,256,128]{2,1,0:T(8,128)S(1)})) conditional(s32[]{:T(128)} %convert_element_type.54, (f32[4,256]{1,0:T(4,128)S(1)}, f32[4,256]{1,0:T(4,128)S(1)}, f32[4,256,128]{2,1,0:T(8,128)S(1)}) %tuple.42, (pred[256,512]{0,1:T(8,128)(4,1)S(1)}, ...), branch_computations={%region_12.12_spmd, %region_13.15_spmd} | conditional | flops 275515392 | bytes 8847396 | solution.py:108
  201.7 1.0 dynamic-slice_bitcast_fusion
  203.8 0.9 convolution_add_fusion
  206.2 2.9 %conditional.2 = ((f32[4,256]{1,0:T(4,128)S(1)}, f32[4,256]{1,0:T(4,128)S(1)}, f32[4,256,128]{2,1,0:T(8,128)S(1)})) conditional(s32[]{:T(128)} %convert_element_type.54, (f32[4,256]{1,0:T(4,128)S(1)}, f32[4,256]{1,0:T(4,128)S(1)}, f32[4,256,128]{2,1,0:T(8,128)S(1)}) %tuple.42, (pred[256,512]{0,1:T(8,128)(4,1)S(1)}, ...), branch_computations={%region_12.12_spmd, %region_13.15_spmd} | conditional | flops 275515392 | bytes 8847396 | solution.py:108
  206.2 1.0 dynamic-slice_bitcast_fusion
  210.7 2.9 %conditional.2 = ((f32[4,256]{1,0:T(4,128)S(1)}, f32[4,256]{1,0:T(4,128)S(1)}, f32[4,256,128]{2,1,0:T(8,128)S(1)})) conditional(s32[]{:T(128)} %convert_element_type.54, (f32[4,256]{1,0:T(4,128)S(1)}, f32[4,256]{1,0:T(4,128)S(1)}, f32[4,256,128]{2,1,0:T(8,128)S(1)}) %tuple.42, (pred[256,512]{0,1:T(8,128)(4,1)S(1)}, ...), branch_computations={%region_12.12_spmd, %region_13.15_spmd} | conditional | flops 275515392 | bytes 8847396 | solution.py:108
  210.7 1.0 dynamic-slice_bitcast_fusion
  215.2 2.9 %conditional.2 = ((f32[4,256]{1,0:T(4,128)S(1)}, f32[4,256]{1,0:T(4,128)S(1)}, f32[4,256,128]{2,1,0:T(8,128)S(1)})) conditional(s32[]{:T(128)} %convert_element_type.54, (f32[4,256]{1,0:T(4,128)S(1)}, f32[4,256]{1,0:T(4,128)S(1)}, f32[4,256,128]{2,1,0:T(8,128)S(1)}) %tuple.42, (pred[256,512]{0,1:T(8,128)(4,1)S(1)}, ...), branch_computations={%region_12.12_spmd, %region_13.15_spmd} | conditional | flops 275515392 | bytes 8847396 | solution.py:108
  215.2 1.0 dynamic-slice_bitcast_fusion
  219.6 2.9 %conditional.2 = ((f32[4,256]{1,0:T(4,128)S(1)}, f32[4,256]{1,0:T(4,128)S(1)}, f32[4,256,128]{2,1,0:T(8,128)S(1)})) conditional(s32[]{:T(128)} %convert_element_type.54, (f32[4,256]{1,0:T(4,128)S(1)}, f32[4,256]{1,0:T(4,128)S(1)}, f32[4,256,128]{2,1,0:T(8,128)S(1)}) %tuple.42, (pred[256,512]{0,1:T(8,128)(4,1)S(1)}, ...), branch_computations={%region_12.12_spmd, %region_13.15_spmd} | conditional | flops 275515392 | bytes 8847396 | solution.py:108
  219.7 1.0 dynamic-slice_bitcast_fusion
  224.1 2.9 %conditional.2 = ((f32[4,256]{1,0:T(4,128)S(1)}, f32[4,256]{1,0:T(4,128)S(1)}, f32[4,256,128]{2,1,0:T(8,128)S(1)})) conditional(s32[]{:T(128)} %convert_element_type.54, (f32[4,256]{1,0:T(4,128)S(1)}, f32[4,256]{1,0:T(4,128)S(1)}, f32[4,256,128]{2,1,0:T(8,128)S(1)}) %tuple.42, (pred[256,512]{0,1:T(8,128)(4,1)S(1)}, ...), branch_computations={%region_12.12_spmd, %region_13.15_spmd} | conditional | flops 275515392 | bytes 8847396 | solution.py:108
  224.1 1.0 dynamic-slice_bitcast_fusion
  228.6 2.9 %conditional.2 = ((f32[4,256]{1,0:T(4,128)S(1)}, f32[4,256]{1,0:T(4,128)S(1)}, f32[4,256,128]{2,1,0:T(8,128)S(1)})) conditional(s32[]{:T(128)} %convert_element_type.54, (f32[4,256]{1,0:T(4,128)S(1)}, f32[4,256]{1,0:T(4,128)S(1)}, f32[4,256,128]{2,1,0:T(8,128)S(1)}) %tuple.42, (pred[256,512]{0,1:T(8,128)(4,1)S(1)}, ...), branch_computations={%region_12.12_spmd, %region_13.15_spmd} | conditional | flops 275515392 | bytes 8847396 | solution.py:108
  228.6 1.0 dynamic-slice_bitcast_fusion
  233.1 2.9 %conditional.2 = ((f32[4,256]{1,0:T(4,128)S(1)}, f32[4,256]{1,0:T(4,128)S(1)}, f32[4,256,128]{2,1,0:T(8,128)S(1)})) conditional(s32[]{:T(128)} %convert_element_type.54, (f32[4,256]{1,0:T(4,128)S(1)}, f32[4,256]{1,0:T(4,128)S(1)}, f32[4,256,128]{2,1,0:T(8,128)S(1)}) %tuple.42, (pred[256,512]{0,1:T(8,128)(4,1)S(1)}, ...), branch_computations={%region_12.12_spmd, %region_13.15_spmd} | conditional | flops 275515392 | bytes 8847396 | solution.py:108
  233.1 1.0 dynamic-slice_bitcast_fusion
  237.6 2.9 %conditional.2 = ((f32[4,256]{1,0:T(4,128)S(1)}, f32[4,256]{1,0:T(4,128)S(1)}, f32[4,256,128]{2,1,0:T(8,128)S(1)})) conditional(s32[]{:T(128)} %convert_element_type.54, (f32[4,256]{1,0:T(4,128)S(1)}, f32[4,256]{1,0:T(4,128)S(1)}, f32[4,256,128]{2,1,0:T(8,128)S(1)}) %tuple.42, (pred[256,512]{0,1:T(8,128)(4,1)S(1)}, ...), branch_computations={%region_12.12_spmd, %region_13.15_spmd} | conditional | flops 275515392 | bytes 8847396 | solution.py:108
  237.6 1.0 dynamic-slice_bitcast_fusion
  242.0 2.9 %conditional.2 = ((f32[4,256]{1,0:T(4,128)S(1)}, f32[4,256]{1,0:T(4,128)S(1)}, f32[4,256,128]{2,1,0:T(8,128)S(1)})) conditional(s32[]{:T(128)} %convert_element_type.54, (f32[4,256]{1,0:T(4,128)S(1)}, f32[4,256]{1,0:T(4,128)S(1)}, f32[4,256,128]{2,1,0:T(8,128)S(1)}) %tuple.42, (pred[256,512]{0,1:T(8,128)(4,1)S(1)}, ...), branch_computations={%region_12.12_spmd, %region_13.15_spmd} | conditional | flops 275515392 | bytes 8847396 | solution.py:108
  242.1 1.0 dynamic-slice_bitcast_fusion
  246.5 2.9 %conditional.2 = ((f32[4,256]{1,0:T(4,128)S(1)}, f32[4,256]{1,0:T(4,128)S(1)}, f32[4,256,128]{2,1,0:T(8,128)S(1)})) conditional(s32[]{:T(128)} %convert_element_type.54, (f32[4,256]{1,0:T(4,128)S(1)}, f32[4,256]{1,0:T(4,128)S(1)}, f32[4,256,128]{2,1,0:T(8,128)S(1)}) %tuple.42, (pred[256,512]{0,1:T(8,128)(4,1)S(1)}, ...), branch_computations={%region_12.12_spmd, %region_13.15_spmd} | conditional | flops 275515392 | bytes 8847396 | solution.py:108
  246.5 1.0 dynamic-slice_bitcast_fusion
  251.0 2.9 %conditional.2 = ((f32[4,256]{1,0:T(4,128)S(1)}, f32[4,256]{1,0:T(4,128)S(1)}, f32[4,256,128]{2,1,0:T(8,128)S(1)})) conditional(s32[]{:T(128)} %convert_element_type.54, (f32[4,256]{1,0:T(4,128)S(1)}, f32[4,256]{1,0:T(4,128)S(1)}, f32[4,256,128]{2,1,0:T(8,128)S(1)}) %tuple.42, (pred[256,512]{0,1:T(8,128)(4,1)S(1)}, ...), branch_computations={%region_12.12_spmd, %region_13.15_spmd} | conditional | flops 275515392 | bytes 8847396 | solution.py:108
  251.0 1.0 dynamic-slice_bitcast_fusion
  255.5 2.9 %conditional.2 = ((f32[4,256]{1,0:T(4,128)S(1)}, f32[4,256]{1,0:T(4,128)S(1)}, f32[4,256,128]{2,1,0:T(8,128)S(1)})) conditional(s32[]{:T(128)} %convert_element_type.54, (f32[4,256]{1,0:T(4,128)S(1)}, f32[4,256]{1,0:T(4,128)S(1)}, f32[4,256,128]{2,1,0:T(8,128)S(1)}) %tuple.42, (pred[256,512]{0,1:T(8,128)(4,1)S(1)}, ...), branch_computations={%region_12.12_spmd, %region_13.15_spmd} | conditional | flops 275515392 | bytes 8847396 | solution.py:108
  255.5 1.0 dynamic-slice_bitcast_fusion
  260.0 2.9 %conditional.2 = ((f32[4,256]{1,0:T(4,128)S(1)}, f32[4,256]{1,0:T(4,128)S(1)}, f32[4,256,128]{2,1,0:T(8,128)S(1)})) conditional(s32[]{:T(128)} %convert_element_type.54, (f32[4,256]{1,0:T(4,128)S(1)}, f32[4,256]{1,0:T(4,128)S(1)}, f32[4,256,128]{2,1,0:T(8,128)S(1)}) %tuple.42, (pred[256,512]{0,1:T(8,128)(4,1)S(1)}, ...), branch_computations={%region_12.12_spmd, %region_13.15_spmd} | conditional | flops 275515392 | bytes 8847396 | solution.py:108
  260.0 1.0 dynamic-slice_bitcast_fusion
  264.4 2.9 %conditional.2 = ((f32[4,256]{1,0:T(4,128)S(1)}, f32[4,256]{1,0:T(4,128)S(1)}, f32[4,256,128]{2,1,0:T(8,128)S(1)})) conditional(s32[]{:T(128)} %convert_element_type.54, (f32[4,256]{1,0:T(4,128)S(1)}, f32[4,256]{1,0:T(4,128)S(1)}, f32[4,256,128]{2,1,0:T(8,128)S(1)}) %tuple.42, (pred[256,512]{0,1:T(8,128)(4,1)S(1)}, ...), branch_computations={%region_12.12_spmd, %region_13.15_spmd} | conditional | flops 275515392 | bytes 8847396 | solution.py:108
  264.5 1.0 dynamic-slice_bitcast_fusion
  267.4 0.9 copy_bitcast_fusion
  (179 shorter events, 49.1 us)
Async XLA Ops:
  6.5 61.3 %all-gather.3.cloned.1.call-start = ((), (), s32[]{:S(2)}) async-start(), calls=%async_computation.1 | async-start | bytes 4718592 | tf_op jit(solution)/shard_map/all_gather | solution.py:33
  67.8 7.1 %copy-start.2 = (bf16[8192,256]{1,0:T(8,128)(2,1)S(1)}, bf16[8192,256]{1,0:T(8,128)(2,1)}, u32[]{:S(2)}) copy-start(bf16[8192,256]{1,0:T(8,128)(2,1)} %param.11) | copy-start | bytes 12582916
  67.8 7.1 %copy-start.3 = (bf16[256,8192]{1,0:T(8,128)(2,1)S(1)}, bf16[256,8192]{1,0:T(8,128)(2,1)}, u32[]{:S(2)}) copy-start(bf16[256,8192]{1,0:T(8,128)(2,1)} %all-gather.3.cloned.1.call-done) | copy-start | bytes 12582916
  76.2 13.7 %copy-start = (s32[512]{0:T(512)S(1)}, s32[512]{0:T(512)}, u32[]{:S(2)}) copy-start(s32[512]{0:T(512)} %param.13) | copy-start | bytes 6148
  77.2 36.7 %copy-start.1 = (s32[64]{0:T(128)S(1)}, s32[64]{0:T(128)}, u32[]{:S(2)}) copy-start(s32[64]{0:T(128)} %param.12) | copy-start | bytes 772
  79.7 32.9 %all-to-all-start = ((bf16[32,16,768]{2,1,0:T(8,128)(2,1)}), bf16[32,16,768]{2,1,0:T(8,128)(2,1)S(1)}, u32[]{:S(2)}, u32[]{:S(2)}) async-start(bf16[32,16,768]{2,1,0:T(8,128)(2,1)} %scatter_fusion), calls=%async_computation | async-start | bytes 1572864 | tf_op jit(solution)/shard_map/all_to_all | solution.py:43
  89.9 105.8 %all-gather.5.cloned.1.call-start = ((), (), s32[]{:S(2)}) async-start(), calls=%async_computation.2 | async-start | bytes 4325376 | tf_op jit(solution)/shard_map/all_gather | solution.py:64
Sparse Core Ops, SparseCore 0:
  9.1 58.6 all-gather.2
  114.1 81.5 all-gather.4
where the time goes:
time: 276 us; the launch traced here: 275 us
  waiting for transfers between devices  100 us (36%)
  local copies, waits for them, and re-layouts  75.3 us (27%)
  other arithmetic  33.8 us (12%)
  matrix products  30.3 us (11%)
  between operations  13.6 us (5%)
  loops' own time  11.6 us (4%)
  starting transfers between devices  10.2 us (4%)
    all_gather x1, waiting for transfers between devices, body(): piece = lax.all_gather(tokens, 'tp', axis=0, tiled=True)  59.6 us
    gather x2, local copies, waits for them, and re-layouts, token_places(): block_order[row_index // block_len] * block_len + row_index % block_len  53.2 us
    all_gather x1, waiting for transfers between devices, body(): key_piece = lax.all_gather(keyvals, 'ctx', axis=0, tiled=True)  23.5 us
    all_to_all x1, waiting for transfers between devices, body(): lax.all_to_all(jnp.zeros((cycle_count, block_len, columns), projected.dty...  16.5 us
    squeeze x16, local copies, waits for them, and re-layouts, body(): finished, unused = lax.scan(advance, initial, stacked)  15.6 us
    dot_general x16, matrix products, update(): jnp.einsum('hqk,kd->hqd', weights.astype(jnp.bfloat16), keyval[:, head_di...  13.9 us
    reduce_or x16, other arithmetic, advance(): return (lax.cond(jnp.any(allowed), update, unchanged, partial_value), None)  13.4 us
    another operation x1, loops' own time, body(): finished, unused = lax.scan(advance, initial, stacked)  10.9 us
  transfers between devices with their start and end apart: 3, of which 3 were waited for; matrix products, arithmetic and copies ran while one was open for 24% of the time, Pallas kernels for 0%

commit v1 on v0

--- a/solution.py
+++ b/solution.py
@@ -30,7 +30,8 @@
     doc_ends = jnp.cumsum(doc_lengths)
     owner_grid = owners.reshape(cycle_count, per_device)
     own_targets = lax.dynamic_index_in_dim(owner_grid, device, 0, keepdims=False)
-    piece = lax.all_gather(tokens, "tp", axis=0, tiled=True)
+    sent = jnp.stack([tokens] * lax.axis_size("tp"))
+    piece = jnp.concatenate(lax.all_to_all(sent, "tp", 0, 0), axis=0)
     query_part = jnp.dot(piece, query_weight, preferred_element_type=jnp.float32).astype(
         jnp.bfloat16
     )

time: 276 us -> 292 us (1.058)
  starting transfers between devices: 10.2 us -> 17.7 us
  waiting for transfers between devices: 100 us -> 104 us
    all_gather x1 -> x0, waiting for transfers between devices: 59.6 us -> none  [body(): piece = lax.all_gather(tokens, 'tp', axis=0, tiled=True)]
    all_to_all x0 -> x1, waiting for transfers between devices: none -> 49.4 us  [body(): piece = jnp.concatenate(lax.all_to_all(sent, 'tp', 0, 0), axis=0)]
    all_gather x1, waiting for transfers between devices: 23.5 us -> 37.8 us  [body(): key_piece = lax.all_gather(keyvals, 'ctx', axis=0, tiled=True)]
    all_to_all x0 -> x1, starting transfers between devices: none -> 5.98 us  [body(): piece = jnp.concatenate(lax.all_to_all(sent, 'tp', 0, 0), axis=0)]
    another operation x3 -> x4, local copies, waits for them, and re-layouts: 0.3 us -> 3.8 us  [the longest x1 3.5 us: body(): sent = jnp.stack([tokens] * lax.axis_size('tp'))]
  transfers between devices with their start and end apart: 3 -> 3, of which waited for: 3 -> 3; matrix products, arithmetic and copies ran while one was open for 24% -> 22% of each run, Pallas kernels for 0% -> 0%
where the time goes in v1:
time: 292 us; the launch traced here: 291 us
  waiting for transfers between devices  104 us (36%)
  local copies, waits for them, and re-layouts  78.1 us (27%)
  other arithmetic  33.8 us (12%)
  matrix products  32.5 us (11%)
  starting transfers between devices  17.7 us (6%)
  between operations  13.6 us (5%)
  loops' own time  11.6 us (4%)
    gather x2, local copies, waits for them, and re-layouts, token_places(): block_order[row_index // block_len] * block_len + row_index % block_len  53.2 us
    all_to_all x1, waiting for transfers between devices, body(): piece = jnp.concatenate(lax.all_to_all(sent, 'tp', 0, 0), axis=0)  49.4 us
    all_gather x1, waiting for transfers between devices, body(): key_piece = lax.all_gather(keyvals, 'ctx', axis=0, tiled=True)  37.8 us
    all_to_all x1, waiting for transfers between devices, body(): lax.all_to_all(jnp.zeros((cycle_count, block_len, columns), projected.dty...  16.5 us
    squeeze x16, local copies, waits for them, and re-layouts, body(): finished, unused = lax.scan(advance, initial, stacked)  15.6 us
    dot_general x16, matrix products, update(): jnp.einsum('hqk,kd->hqd', weights.astype(jnp.bfloat16), keyval[:, head_di...  13.9 us
    reduce_or x16, other arithmetic, advance(): return (lax.cond(jnp.any(allowed), update, unchanged, partial_value), None)  13.4 us
    all_to_all x1, starting transfers between devices, body(): lax.all_to_all(jnp.zeros((cycle_count, block_len, columns), projected.dty...  11.7 us
  transfers between devices with their start and end apart: 3, of which 3 were waited for; matrix products, arithmetic and copies ran while one was open for 22% of the time, Pallas kernels for 0%

profile of v1, /device:TPU:1, one launch (start us, length us, event | category | flops | bytes accessed | tf_op | source)
XLA Modules:
  0.0 291.0 jit_solution(3404569222870240396)
XLA Ops:
  6.5 3.5 %stack.2 = bf16[8,32,8192]{2,1,0:T(8,128)(2,1)} broadcast(bf16[32,8192]{1,0:T(8,128)(2,1)} %param.9), dimensions={1,2} | broadcast | bytes 4718592 | tf_op jit(solution)/shard_map/stack | solution.py:33
  10.0 6.0 %all-to-all-start = ((bf16[8,32,8192]{2,1,0:T(8,128)(2,1)}), bf16[8,32,8192]{2,1,0:T(8,128)(2,1)}, u32[]{:S(2)}, u32[]{:S(2)}) async-start(bf16[8,32,8192]{2,1,0:T(8,128)(2,1)} %stack.2), calls=%async_computation | async-start | bytes 8388608 | tf_op jit(solution)/shard_map/all_to_all | solution.py:34
  16.3 49.4 %all-to-all-done = bf16[8,32,8192]{2,1,0:T(8,128)(2,1)} async-done(((bf16[8,32,8192]{2,1,0:T(8,128)(2,1)}), bf16[8,32,8192]{2,1,0:T(8,128)(2,1)}, u32[]{:S(2)}, u32[]{:S(2)}) %all-to-all-start) | async-done | bytes 4194336 | tf_op jit(solution)/shard_map/all_to_all | solution.py:34
  65.7 7.1 %convolution_convert_fusion = bf16[256,512]{1,0:T(8,128)(2,1)S(1)} fusion(bf16[256,8192]{1,0:T(8,128)(2,1)} %bitcast.10, bf16[8192,512]{1,0:T(8,128)(2,1)} %param.10), kind=kOutput, calls=%fused_computation.28 | convolution fusion | flops 2147614720 | bytes 12845056 | tf_op jit(solution)/shard_map/dot_general | solution.py:35
  72.8 3.4 %convolution_convert_fusion.1 = bf16[256,256]{1,0:T(8,128)(2,1)S(1)} fusion(bf16[256,8192]{1,0:T(8,128)(2,1)} %bitcast.10, bf16[8192,256]{1,0:T(8,128)(2,1)S(1)} %copy-done.2), kind=kOutput, calls=%fused_computation.29 | convolution fusion | flops 1073807360 | bytes 8519680 | tf_op jit(solution)/shard_map/dot_general | solution.py:38
  76.3 0.9 broadcast_in_dim.60
  77.2 2.5 scatter_fusion
  79.8 11.7 %all-to-all-start.1 = ((bf16[32,16,768]{2,1,0:T(8,128)(2,1)}), bf16[32,16,768]{2,1,0:T(8,128)(2,1)S(1)}, u32[]{:S(2)}, u32[]{:S(2)}) async-start(bf16[32,16,768]{2,1,0:T(8,128)(2,1)} %scatter_fusion), calls=%async_computation.1 | async-start | bytes 1572864 | tf_op jit(solution)/shard_map/all_to_all | solution.py:44
  92.8 4.1 %scatter_custom_fusion.1 = s32[16]{0:T(128)S(1)} fusion(s32[512]{0:T(512)S(1)} %bitcast.64, s32[512]{0:T(512)S(1)} %broadcast.400, s32[]{:T(128)} %copy.68), kind=kCustom, calls=%fused_computation.89 | custom fusion | flops 512 | bytes 68 | tf_op jit(solution)/shard_map/scatter-add | solution.py:51
  97.8 16.5 %all-to-all-done.1 = bf16[32,16,768]{2,1,0:T(8,128)(2,1)S(1)} async-done(((bf16[32,16,768]{2,1,0:T(8,128)(2,1)}), bf16[32,16,768]{2,1,0:T(8,128)(2,1)S(1)}, u32[]{:S(2)}, u32[]{:S(2)}) %all-to-all-start.1) | async-done | bytes 786464 | tf_op jit(solution)/shard_map/all_to_all | solution.py:44
  115.9 3.8 %sort.17 = (s32[512]{0:T(512)}, s32[512]{0:T(512)S(1)}) sort(s32[512]{0:T(512)S(1)} %copy-done, s32[512]{0:T(512)S(1)} %iota.37), dimensions={0}, to_apply=%region_6.7 | sort | flops 4608 | bytes 8192 | tf_op jit(solution)/shard_map/jit(argsort)/sort | solution.py:29
  119.7 1.9 gather_fusion.1
  121.7 51.2 %gather_fusion = s32[8192]{0:T(1024)S(1)} fusion(s32[512]{0:T(512)S(1)} %get-tuple-element.106, s32[8192]{0:T(1024)S(1)} %broadcast_clamp_fusion), kind=kCustom, calls=%fused_computation | custom fusion | bytes 98304 | tf_op jit(solution)/shard_map/gather | solution.py:12
  173.8 37.8 %all-gather.2.cloned.1.call-done = bf16[8192,256]{1,0:T(8,128)(2,1)} async-done(((bf16[256,256]{1,0:T(8,128)(2,1)}), bf16[8192,256]{1,0:T(8,128)(2,1)}) %all-gather.2.cloned.1.call-update) | async-done | bytes 4194320 | tf_op jit(solution)/shard_map/all_gather | solution.py:65
  211.6 71.7 %while.14 = (s32[]{:T(128)}, f32[4,256]{1,0:T(4,128)S(1)}, f32[4,256]{1,0:T(4,128)S(1)}, f32[4,256,128]{2,1,0:T(8,128)S(1)}, s32[16,512]{1,0:T(8,128)S(1)}, /*in...) while((s32[]{:T(128)}, f32[4,256]{1,0:T(4,128)S(1)}, ...), condition=%wide.region_16.17_spmd, body=%wide.region_10.16_spmd.sunk | while | flops 276039680 | bytes 8993003 | solution.py:111
  213.1 2.9 %conditional.2 = ((f32[4,256]{1,0:T(4,128)S(1)}, f32[4,256]{1,0:T(4,128)S(1)}, f32[4,256,128]{2,1,0:T(8,128)S(1)})) conditional(s32[]{:T(128)} %convert_element_type.54, (f32[4,256]{1,0:T(4,128)S(1)}, f32[4,256]{1,0:T(4,128)S(1)}, f32[4,256,128]{2,1,0:T(8,128)S(1)}) %tuple.42, (pred[256,512]{0,1:T(8,128)(4,1)S(1)}, ...), branch_computations={%region_12.12_spmd, %region_13.15_spmd} | conditional | flops 275515392 | bytes 8847396 | solution.py:109
  213.1 1.0 dynamic-slice_bitcast_fusion
  217.6 2.9 %conditional.2 = ((f32[4,256]{1,0:T(4,128)S(1)}, f32[4,256]{1,0:T(4,128)S(1)}, f32[4,256,128]{2,1,0:T(8,128)S(1)})) conditional(s32[]{:T(128)} %convert_element_type.54, (f32[4,256]{1,0:T(4,128)S(1)}, f32[4,256]{1,0:T(4,128)S(1)}, f32[4,256,128]{2,1,0:T(8,128)S(1)}) %tuple.42, (pred[256,512]{0,1:T(8,128)(4,1)S(1)}, ...), branch_computations={%region_12.12_spmd, %region_13.15_spmd} | conditional | flops 275515392 | bytes 8847396 | solution.py:109
  217.6 1.0 dynamic-slice_bitcast_fusion
  222.1 2.9 %conditional.2 = ((f32[4,256]{1,0:T(4,128)S(1)}, f32[4,256]{1,0:T(4,128)S(1)}, f32[4,256,128]{2,1,0:T(8,128)S(1)})) conditional(s32[]{:T(128)} %convert_element_type.54, (f32[4,256]{1,0:T(4,128)S(1)}, f32[4,256]{1,0:T(4,128)S(1)}, f32[4,256,128]{2,1,0:T(8,128)S(1)}) %tuple.42, (pred[256,512]{0,1:T(8,128)(4,1)S(1)}, ...), branch_computations={%region_12.12_spmd, %region_13.15_spmd} | conditional | flops 275515392 | bytes 8847396 | solution.py:109
  222.1 1.0 dynamic-slice_bitcast_fusion
  226.6 2.9 %conditional.2 = ((f32[4,256]{1,0:T(4,128)S(1)}, f32[4,256]{1,0:T(4,128)S(1)}, f32[4,256,128]{2,1,0:T(8,128)S(1)})) conditional(s32[]{:T(128)} %convert_element_type.54, (f32[4,256]{1,0:T(4,128)S(1)}, f32[4,256]{1,0:T(4,128)S(1)}, f32[4,256,128]{2,1,0:T(8,128)S(1)}) %tuple.42, (pred[256,512]{0,1:T(8,128)(4,1)S(1)}, ...), branch_computations={%region_12.12_spmd, %region_13.15_spmd} | conditional | flops 275515392 | bytes 8847396 | solution.py:109
  226.6 1.0 dynamic-slice_bitcast_fusion
  231.0 2.9 %conditional.2 = ((f32[4,256]{1,0:T(4,128)S(1)}, f32[4,256]{1,0:T(4,128)S(1)}, f32[4,256,128]{2,1,0:T(8,128)S(1)})) conditional(s32[]{:T(128)} %convert_element_type.54, (f32[4,256]{1,0:T(4,128)S(1)}, f32[4,256]{1,0:T(4,128)S(1)}, f32[4,256,128]{2,1,0:T(8,128)S(1)}) %tuple.42, (pred[256,512]{0,1:T(8,128)(4,1)S(1)}, ...), branch_computations={%region_12.12_spmd, %region_13.15_spmd} | conditional | flops 275515392 | bytes 8847396 | solution.py:109
  231.1 1.0 dynamic-slice_bitcast_fusion
  235.5 2.9 %conditional.2 = ((f32[4,256]{1,0:T(4,128)S(1)}, f32[4,256]{1,0:T(4,128)S(1)}, f32[4,256,128]{2,1,0:T(8,128)S(1)})) conditional(s32[]{:T(128)} %convert_element_type.54, (f32[4,256]{1,0:T(4,128)S(1)}, f32[4,256]{1,0:T(4,128)S(1)}, f32[4,256,128]{2,1,0:T(8,128)S(1)}) %tuple.42, (pred[256,512]{0,1:T(8,128)(4,1)S(1)}, ...), branch_computations={%region_12.12_spmd, %region_13.15_spmd} | conditional | flops 275515392 | bytes 8847396 | solution.py:109
  235.5 1.0 dynamic-slice_bitcast_fusion
  240.0 2.9 %conditional.2 = ((f32[4,256]{1,0:T(4,128)S(1)}, f32[4,256]{1,0:T(4,128)S(1)}, f32[4,256,128]{2,1,0:T(8,128)S(1)})) conditional(s32[]{:T(128)} %convert_element_type.54, (f32[4,256]{1,0:T(4,128)S(1)}, f32[4,256]{1,0:T(4,128)S(1)}, f32[4,256,128]{2,1,0:T(8,128)S(1)}) %tuple.42, (pred[256,512]{0,1:T(8,128)(4,1)S(1)}, ...), branch_computations={%region_12.12_spmd, %region_13.15_spmd} | conditional | flops 275515392 | bytes 8847396 | solution.py:109
  240.0 1.0 dynamic-slice_bitcast_fusion
  244.5 2.9 %conditional.2 = ((f32[4,256]{1,0:T(4,128)S(1)}, f32[4,256]{1,0:T(4,128)S(1)}, f32[4,256,128]{2,1,0:T(8,128)S(1)})) conditional(s32[]{:T(128)} %convert_element_type.54, (f32[4,256]{1,0:T(4,128)S(1)}, f32[4,256]{1,0:T(4,128)S(1)}, f32[4,256,128]{2,1,0:T(8,128)S(1)}) %tuple.42, (pred[256,512]{0,1:T(8,128)(4,1)S(1)}, ...), branch_computations={%region_12.12_spmd, %region_13.15_spmd} | conditional | flops 275515392 | bytes 8847396 | solution.py:109
  244.5 1.0 dynamic-slice_bitcast_fusion
  249.0 2.9 %conditional.2 = ((f32[4,256]{1,0:T(4,128)S(1)}, f32[4,256]{1,0:T(4,128)S(1)}, f32[4,256,128]{2,1,0:T(8,128)S(1)})) conditional(s32[]{:T(128)} %convert_element_type.54, (f32[4,256]{1,0:T(4,128)S(1)}, f32[4,256]{1,0:T(4,128)S(1)}, f32[4,256,128]{2,1,0:T(8,128)S(1)}) %tuple.42, (pred[256,512]{0,1:T(8,128)(4,1)S(1)}, ...), branch_computations={%region_12.12_spmd, %region_13.15_spmd} | conditional | flops 275515392 | bytes 8847396 | solution.py:109
  249.0 1.0 dynamic-slice_bitcast_fusion
  253.4 2.9 %conditional.2 = ((f32[4,256]{1,0:T(4,128)S(1)}, f32[4,256]{1,0:T(4,128)S(1)}, f32[4,256,128]{2,1,0:T(8,128)S(1)})) conditional(s32[]{:T(128)} %convert_element_type.54, (f32[4,256]{1,0:T(4,128)S(1)}, f32[4,256]{1,0:T(4,128)S(1)}, f32[4,256,128]{2,1,0:T(8,128)S(1)}) %tuple.42, (pred[256,512]{0,1:T(8,128)(4,1)S(1)}, ...), branch_computations={%region_12.12_spmd, %region_13.15_spmd} | conditional | flops 275515392 | bytes 8847396 | solution.py:109
  253.5 1.0 dynamic-slice_bitcast_fusion
  257.9 2.9 %conditional.2 = ((f32[4,256]{1,0:T(4,128)S(1)}, f32[4,256]{1,0:T(4,128)S(1)}, f32[4,256,128]{2,1,0:T(8,128)S(1)})) conditional(s32[]{:T(128)} %convert_element_type.54, (f32[4,256]{1,0:T(4,128)S(1)}, f32[4,256]{1,0:T(4,128)S(1)}, f32[4,256,128]{2,1,0:T(8,128)S(1)}) %tuple.42, (pred[256,512]{0,1:T(8,128)(4,1)S(1)}, ...), branch_computations={%region_12.12_spmd, %region_13.15_spmd} | conditional | flops 275515392 | bytes 8847396 | solution.py:109
  257.9 1.0 dynamic-slice_bitcast_fusion
  262.4 2.9 %conditional.2 = ((f32[4,256]{1,0:T(4,128)S(1)}, f32[4,256]{1,0:T(4,128)S(1)}, f32[4,256,128]{2,1,0:T(8,128)S(1)})) conditional(s32[]{:T(128)} %convert_element_type.54, (f32[4,256]{1,0:T(4,128)S(1)}, f32[4,256]{1,0:T(4,128)S(1)}, f32[4,256,128]{2,1,0:T(8,128)S(1)}) %tuple.42, (pred[256,512]{0,1:T(8,128)(4,1)S(1)}, ...), branch_computations={%region_12.12_spmd, %region_13.15_spmd} | conditional | flops 275515392 | bytes 8847396 | solution.py:109
  262.4 1.0 dynamic-slice_bitcast_fusion
  266.9 2.9 %conditional.2 = ((f32[4,256]{1,0:T(4,128)S(1)}, f32[4,256]{1,0:T(4,128)S(1)}, f32[4,256,128]{2,1,0:T(8,128)S(1)})) conditional(s32[]{:T(128)} %convert_element_type.54, (f32[4,256]{1,0:T(4,128)S(1)}, f32[4,256]{1,0:T(4,128)S(1)}, f32[4,256,128]{2,1,0:T(8,128)S(1)}) %tuple.42, (pred[256,512]{0,1:T(8,128)(4,1)S(1)}, ...), branch_computations={%region_12.12_spmd, %region_13.15_spmd} | conditional | flops 275515392 | bytes 8847396 | solution.py:109
  266.9 1.0 dynamic-slice_bitcast_fusion
  271.4 2.9 %conditional.2 = ((f32[4,256]{1,0:T(4,128)S(1)}, f32[4,256]{1,0:T(4,128)S(1)}, f32[4,256,128]{2,1,0:T(8,128)S(1)})) conditional(s32[]{:T(128)} %convert_element_type.54, (f32[4,256]{1,0:T(4,128)S(1)}, f32[4,256]{1,0:T(4,128)S(1)}, f32[4,256,128]{2,1,0:T(8,128)S(1)}) %tuple.42, (pred[256,512]{0,1:T(8,128)(4,1)S(1)}, ...), branch_computations={%region_12.12_spmd, %region_13.15_spmd} | conditional | flops 275515392 | bytes 8847396 | solution.py:109
  271.4 1.0 dynamic-slice_bitcast_fusion
  275.8 2.9 %conditional.2 = ((f32[4,256]{1,0:T(4,128)S(1)}, f32[4,256]{1,0:T(4,128)S(1)}, f32[4,256,128]{2,1,0:T(8,128)S(1)})) conditional(s32[]{:T(128)} %convert_element_type.54, (f32[4,256]{1,0:T(4,128)S(1)}, f32[4,256]{1,0:T(4,128)S(1)}, f32[4,256,128]{2,1,0:T(8,128)S(1)}) %tuple.42, (pred[256,512]{0,1:T(8,128)(4,1)S(1)}, ...), branch_computations={%region_12.12_spmd, %region_13.15_spmd} | conditional | flops 275515392 | bytes 8847396 | solution.py:109
  275.9 1.0 dynamic-slice_bitcast_fusion
  280.3 2.9 %conditional.2 = ((f32[4,256]{1,0:T(4,128)S(1)}, f32[4,256]{1,0:T(4,128)S(1)}, f32[4,256,128]{2,1,0:T(8,128)S(1)})) conditional(s32[]{:T(128)} %convert_element_type.54, (f32[4,256]{1,0:T(4,128)S(1)}, f32[4,256]{1,0:T(4,128)S(1)}, f32[4,256,128]{2,1,0:T(8,128)S(1)}) %tuple.42, (pred[256,512]{0,1:T(8,128)(4,1)S(1)}, ...), branch_computations={%region_12.12_spmd, %region_13.15_spmd} | conditional | flops 275515392 | bytes 8847396 | solution.py:109
  280.3 1.0 dynamic-slice_bitcast_fusion
  283.3 0.9 copy_bitcast_fusion
  (177 shorter events, 49.4 us)
Async XLA Ops:
  10.0 6.0 %copy-start = (s32[512]{0:T(512)S(1)}, s32[512]{0:T(512)}, u32[]{:S(2)}) copy-start(s32[512]{0:T(512)} %param.13) | copy-start | bytes 6148
  10.0 55.7 %all-to-all-start = ((bf16[8,32,8192]{2,1,0:T(8,128)(2,1)}), bf16[8,32,8192]{2,1,0:T(8,128)(2,1)}, u32[]{:S(2)}, u32[]{:S(2)}) async-start(bf16[8,32,8192]{2,1,0:T(8,128)(2,1)} %stack.2), calls=%async_computation | async-start | bytes 8388608 | tf_op jit(solution)/shard_map/all_to_all | solution.py:34
  65.7 7.1 %copy-start.2 = (bf16[8192,256]{1,0:T(8,128)(2,1)S(1)}, bf16[8192,256]{1,0:T(8,128)(2,1)}, u32[]{:S(2)}) copy-start(bf16[8192,256]{1,0:T(8,128)(2,1)} %param.11) | copy-start | bytes 12582916
  77.2 38.3 %copy-start.1 = (s32[64]{0:T(128)S(1)}, s32[64]{0:T(128)}, u32[]{:S(2)}) copy-start(s32[64]{0:T(128)} %param.12) | copy-start | bytes 772
  79.8 34.5 %all-to-all-start.1 = ((bf16[32,16,768]{2,1,0:T(8,128)(2,1)}), bf16[32,16,768]{2,1,0:T(8,128)(2,1)S(1)}, u32[]{:S(2)}, u32[]{:S(2)}) async-start(bf16[32,16,768]{2,1,0:T(8,128)(2,1)} %scatter_fusion), calls=%async_computation.1 | async-start | bytes 1572864 | tf_op jit(solution)/shard_map/all_to_all | solution.py:44
  91.5 120.0 %all-gather.2.cloned.1.call-start = ((), (), s32[]{:S(2)}) async-start(), calls=%async_computation.2 | async-start | bytes 4325376 | tf_op jit(solution)/shard_map/all_gather | solution.py:65
Sparse Core Ops, SparseCore 0:
  115.7 95.8 all-gather.1
